TPU v7x, 32 devices: a whole 2x2x4 slice. The times are simulated.
32 devices in a mesh: res: 8 (over z, y), seq: 4 (over x, core).
Axes of the slice: x: 2, y: 2, z: 4, core: 2. Of those that a mesh axis runs over, the one named last changes fastest.
Arguments:
- alignment: bfloat16 [384, 256, 256], P('seq', 'res'), may hold values from -6 to 6
- query_weight: bfloat16 [256, 256], replicated, may hold values from -1 to 1
- w_keyval: bfloat16 [256, 512], replicated, may hold values from -0.375 to 0.375
- w_gate: bfloat16 [256, 256], replicated, may hold values from -0.375 to 0.375
- output_weight: bfloat16 [256, 256], replicated, may hold values from -0.75 to 0.75
- w_factors: bfloat16 [256, 64], replicated, may hold values from -1.5 to 1.5
- w_pair_out: bfloat16 [1024, 128], replicated, may hold values from -0.1875 to 0.1875
Outputs:
- alignment_update: bfloat16 [384, 256, 256], P('seq', 'res')
- pair_representation_update: bfloat16 [256, 256, 128], P(('res', 'seq'))
All inputs are finite; a program needn't handle non-finite values.
Results may differ from a plain program's by a relative error of at most 0.012.
The roundings to bfloat16 on the way count: a program that leaves them out, or rounds other values in their place, can miss the bound.
Values may be sent and summed in bfloat16 or wider, within the bound.
A program may use at most 256 MiB of HBM per device.

v0:
```python
import math

import jax
import jax.numpy as jnp
from jax import lax
from jax.sharding import PartitionSpec as P

HEADS = 8
HC = 32


epsilon = 1e-05


def normalize(alignment):
    values = alignment.astype(jnp.float32)
    centered = values - jnp.mean(values, axis=-1, keepdims=True)
    spread = jnp.mean(centered * centered, axis=-1, keepdims=True)
    return (centered * lax.rsqrt(spread + epsilon)).astype(jnp.bfloat16)


def apply_projection(normed, weight):
    return jnp.dot(normed, weight, preferred_element_type=jnp.float32)


def attend_group(query_rows, keyval_rows, running, start_row, group_size):
    denominators, accumulated = running
    hidden = query_rows.shape[2]
    query_slice = lax.dynamic_slice_in_dim(query_rows, start_row, group_size, 1)
    keyval_slice = lax.dynamic_slice_in_dim(keyval_rows, start_row, group_size, 1)
    query_count = query_slice.shape[0]
    key_count = keyval_slice.shape[0]
    per_head_query = query_slice.reshape(query_count, group_size, HEADS, HC)
    head_keys = keyval_slice[:, :, :hidden].reshape(key_count, group_size, HEADS, HC)
    head_values = keyval_slice[:, :, hidden:].reshape(key_count, group_size, HEADS, HC)
    scores = jnp.einsum(
        "qrhd,krhd->rhqk", per_head_query, head_keys, preferred_element_type=jnp.float32
    ) * (1.0 / math.sqrt(HC))
    exponent = jnp.exp(scores)
    weights = exponent.astype(jnp.bfloat16)
    summed = jnp.transpose(jnp.sum(exponent, axis=-1), (2, 0, 1))
    weighted = jnp.einsum(
        "rhqk,krhd->qrhd", weights, head_values, preferred_element_type=jnp.float32
    ).reshape(query_count, group_size, hidden)
    prior_sums = lax.dynamic_slice_in_dim(denominators, start_row, group_size, 1)
    prior_values = lax.dynamic_slice_in_dim(accumulated, start_row, group_size, 1)
    denominators = lax.dynamic_update_slice_in_dim(denominators, prior_sums + summed, start_row, 1)
    accumulated = lax.dynamic_update_slice_in_dim(
        accumulated, prior_values + weighted, start_row, 1
    )
    return (denominators, accumulated)


def attend_piece(query_rows, running, keyval_rows):
    group_size = 4
    group_total = query_rows.shape[1] // group_size

    def one_group(group_index, current):
        return attend_group(query_rows, keyval_rows, current, group_index * group_size, group_size)

    return lax.fori_loop(0, group_total, one_group, running)


def outer_panel(left_rows, right_cols, scaling, pair_weight):
    factor = pair_weight.shape[0]
    row_count = left_rows.shape[1] // factor
    column_total = right_cols.shape[1] // factor
    products = (
        lax.dot_general(
            left_rows, right_cols, (((0,), (0,)), ((), ())), preferred_element_type=jnp.float32
        )
        * scaling
    )
    products = products.reshape(row_count, factor, column_total, factor)
    upper_part = products.astype(jnp.bfloat16)
    lower_part = (products - upper_part.astype(jnp.float32)).astype(jnp.bfloat16)
    upper_terms = jnp.einsum(
        "icje,cep->ijp", upper_part, pair_weight, preferred_element_type=jnp.float32
    )
    lower_terms = jnp.einsum(
        "icje,cep->ijp", lower_part, pair_weight, preferred_element_type=jnp.float32
    )
    return upper_terms + lower_terms


def outer_blocks(left_rows, right_cols, scaling, pair_weight):
    factor = pair_weight.shape[0]
    column_total = right_cols.shape[1] // factor
    panel_width = math.gcd(column_total, 128)
    panel_total = column_total // panel_width

    def one_panel(panel_index):
        column_slice = lax.dynamic_slice_in_dim(
            right_cols, panel_index * panel_width * factor, panel_width * factor, 1
        )
        return outer_panel(left_rows, column_slice, scaling, pair_weight)

    stacked = lax.map(one_panel, jnp.arange(panel_total, dtype=jnp.int32))
    return jnp.transpose(stacked, (1, 0, 2, 3)).reshape(
        stacked.shape[1], column_total, stacked.shape[3]
    )


def per_device(alignment, query_weight, w_keyval, w_gate, output_weight, w_factors, w_pair_out):
    normed = normalize(alignment)
    queries = apply_projection(normed, query_weight).astype(jnp.bfloat16)
    gating = jax.nn.sigmoid(apply_projection(normed, w_gate))
    seq_rows = normed.shape[0]
    residues = normed.shape[1]
    hidden = queries.shape[2]
    totals = (
        jnp.zeros((seq_rows, residues, HEADS), jnp.float32),
        jnp.zeros((seq_rows, residues, hidden), jnp.float32),
    )
    keyvals = apply_projection(lax.all_gather(normed, "seq", axis=0, tiled=True), w_keyval).astype(
        jnp.bfloat16
    )
    denominators, accumulated = attend_piece(queries, totals, keyvals)
    attended = (
        accumulated.reshape(seq_rows, residues, HEADS, HC) / denominators[:, :, :, None]
    ).reshape(seq_rows, residues, hidden)
    gated_output_rows = (gating * attended).astype(jnp.bfloat16)
    alignment_update = apply_projection(gated_output_rows, output_weight).astype(jnp.bfloat16)
    factors = apply_projection(normed, w_factors).astype(jnp.bfloat16)
    factor = factors.shape[2] // 2
    left_factor = factors[:, :, :factor].reshape(seq_rows, residues * factor)
    right_factor = factors[:, :, factor:].reshape(seq_rows, residues * factor)
    pair_weight = w_pair_out.reshape(factor, factor, w_pair_out.shape[1])
    groups = lax.axis_size("seq")
    own_rows = residues // groups
    scaling = 1.0 / (seq_rows * groups)
    left_all, right_all = (
        lax.all_gather(left_factor, "seq", axis=0, tiled=True),
        lax.all_gather(right_factor, "seq", axis=0, tiled=True),
    )
    own_left = lax.dynamic_slice_in_dim(
        left_all, lax.axis_index("seq") * (own_rows * factor), own_rows * factor, 1
    )
    pair_representation_update = outer_blocks(
        own_left, lax.all_gather(right_all, "res", axis=1, tiled=True), scaling, pair_weight
    )
    return (alignment_update, pair_representation_update.astype(jnp.bfloat16))


def solution(mesh):
    in_specs = (P("seq", "res", None), P(), P(), P(), P(), P(), P())
    out_specs = (P("seq", "res", None), P(("res", "seq"), None, None))
    return jax.shard_map(
        per_device, mesh=mesh, in_specs=in_specs, out_specs=out_specs, check_vma=False
    )
```

profile of v0, /device:TPU:0, one launch (start us, length us, event | category | flops | bytes accessed | tf_op | source)
XLA Modules:
  0.0 270.5 jit_solution(1313940980121945734)
XLA Ops:
  7.2 2.5 convert_reduce_fusion
  9.7 2.9 %fusion.21 = f32[96,32]{0,1:T(8,128)S(1)} fusion(f32[96,32]{0,1:T(8,128)S(1)} %broadcast_multiply_fusion, bf16[96,32,256]{2,1,0:T(8,128)(2,1)} %param.11), kind=kLoop, calls=%fused_computation.34 | loop fusion | flops 3142656 | bytes 1597440 | tf_op jit(solution)/shard_map/reduce_sum | solution.py:18
  12.7 3.1 %fusion.22 = bf16[96,32,256]{2,0,1:T(8,128)(2,1)} fusion(f32[96,32]{0,1:T(8,128)S(1)} %add_rsqrt_fusion, f32[96,32]{0,1:T(8,128)S(1)} %broadcast_multiply_fusion, bf16[96,32,256]{2,1,0:T(8,128)(2,1)S(1)} %copy-done.3), kind=kLoop, calls=%fused_computation.35 | loop fusion | flops 3145728 | bytes 3170304 | tf_op jit(solution)/shard_map/convert_element_type | solution.py:19
  15.8 2.6 convolution_convert_fusion.3
  18.7 1.5 copy.75
  20.3 1.1 copy.76
  21.4 11.6 %all_gather.13 = bf16[384,1024]{1,0:T(8,128)(2,1)} all-gather(bf16[96,1024]{1,0:T(8,128)(2,1)S(1)} %copy.76), channel_id=1, replica_groups=mesh['res'=8,'seq'=4] {'seq'}, dimensions={0}, use_global_device_ids=true | all-gather | bytes 983040 | tf_op jit(solution)/shard_map/all_gather | solution.py:134
  33.0 2.3 convolution_convert_fusion.2
  36.3 14.7 %all_gather.15 = bf16[384,1024]{1,0:T(8,128)(2,1)S(1)} all-gather(bf16[96,1024]{1,0:T(8,128)(2,1)S(1)} %copy.78), channel_id=1, replica_groups=mesh['res'=8,'seq'=4] {'seq'}, dimensions={0}, use_global_device_ids=true | all-gather | bytes 983040 | tf_op jit(solution)/shard_map/all_gather | solution.py:133
  51.0 19.1 %all-gather.3.cloned.1.call-done = bf16[384,32,256]{2,0,1:T(8,128)(2,1)} async-done(((bf16[96,32,256]{2,0,1:T(8,128)(2,1)}), bf16[384,32,256]{2,0,1:T(8,128)(2,1)}) %all-gather.3.cloned.1.call-update) | async-done | bytes 6291472 | tf_op jit(solution)/shard_map/all_gather | solution.py:115
  70.2 9.1 %convolution_convert_fusion = bf16[384,32,512]{2,0,1:T(8,128)(2,1)} fusion(bf16[384,32,256]{2,0,1:T(8,128)(2,1)} %all-gather.3.cloned.1.call-done, bf16[256,512]{1,0:T(8,128)(2,1)S(1)} %copy-done), kind=kOutput, calls=%fused_computation.29 | convolution fusion | flops 3227516928 | bytes 19136512 | tf_op jit(solution)/shard_map/dot_general | solution.py:23
  79.2 2.1 broadcast_in_dim.20.clone
  81.3 98.3 %while.27 = (s32[]{:T(128)}, f32[96,32,8]{0,2,1:T(8,128)S(1)}, f32[96,32,256]{2,0,1:T(8,128)}, bf16[96,32,256]{2,1,0:T(8,128)(2,1)}, bf16[384,32,512]{2,0,1:T(8,...) while((s32[]{:T(128)}, f32[96,32,8]{0,2,1:T(8,128)S(1)}, f32[96,32,256]{2,0,1:T(8,128)}, ...), condition=%wide.region_4.0_spmd, body=%wide.region_2.0_spmd.sunk | while | flops 155811840 | bytes 23064760 | solution.py:61
  81.4 1.5 constant_dynamic-slice_fusion.9
  83.3 1.1 constant_dynamic-slice_fusion.8
  84.6 3.2 %fusion.56 = (f32[4,8,96]{2,1,0:T(8,128)S(1)}, f32[4,8,96,384]{3,2,1,0:T(8,128)}) fusion(bf16[96,4,8,32]{0,3,2,1:T(8,128)(2,1)S(1)} %bitcast.100, bf16[384,4,8,32]{0,3,2,1:T(8,128)(2,1)S(1)} %bitcast.98), kind=kOutput, calls=%fused_computation.2.clone.1 | convolution fusion | flops 77853696 | bytes 5713920 | tf_op jit(solution)/shard_map/while/body/eval_jaxpr/qrhd,krhd->rhqk/dot_general | solution.py:36
  88.1 3.3 %fusion.58 = f32[4,8,32,96]{3,2,1,0:T(8,128)S(1)} fusion(bf16[384,4,8,32]{0,3,2,1:T(8,128)(2,1)S(1)} %bitcast.99, f32[4,8,96,384]{3,2,1,0:T(8,128)} %get-tuple-element.305), kind=kOutput, calls=%fused_computation.3.clone.1 | convolution fusion | flops 77856768 | bytes 5898240 | tf_op jit(solution)/shard_map/while/body/eval_jaxpr/rhqk,krhd->qrhd/dot_general | solution.py:42
  91.4 1.0 constant_dynamic-slice_fusion.10
  93.7 1.5 constant_dynamic-slice_fusion.9
  95.6 1.1 constant_dynamic-slice_fusion.8
  96.9 3.2 %fusion.56 = (f32[4,8,96]{2,1,0:T(8,128)S(1)}, f32[4,8,96,384]{3,2,1,0:T(8,128)}) fusion(bf16[96,4,8,32]{0,3,2,1:T(8,128)(2,1)S(1)} %bitcast.100, bf16[384,4,8,32]{0,3,2,1:T(8,128)(2,1)S(1)} %bitcast.98), kind=kOutput, calls=%fused_computation.2.clone.1 | convolution fusion | flops 77853696 | bytes 5713920 | tf_op jit(solution)/shard_map/while/body/eval_jaxpr/qrhd,krhd->rhqk/dot_general | solution.py:36
  100.4 3.3 %fusion.58 = f32[4,8,32,96]{3,2,1,0:T(8,128)S(1)} fusion(bf16[384,4,8,32]{0,3,2,1:T(8,128)(2,1)S(1)} %bitcast.99, f32[4,8,96,384]{3,2,1,0:T(8,128)} %get-tuple-element.305), kind=kOutput, calls=%fused_computation.3.clone.1 | convolution fusion | flops 77856768 | bytes 5898240 | tf_op jit(solution)/shard_map/while/body/eval_jaxpr/rhqk,krhd->qrhd/dot_general | solution.py:42
  103.7 1.0 constant_dynamic-slice_fusion.10
  106.0 1.5 constant_dynamic-slice_fusion.9
  107.8 1.1 constant_dynamic-slice_fusion.8
  109.1 3.2 %fusion.56 = (f32[4,8,96]{2,1,0:T(8,128)S(1)}, f32[4,8,96,384]{3,2,1,0:T(8,128)}) fusion(bf16[96,4,8,32]{0,3,2,1:T(8,128)(2,1)S(1)} %bitcast.100, bf16[384,4,8,32]{0,3,2,1:T(8,128)(2,1)S(1)} %bitcast.98), kind=kOutput, calls=%fused_computation.2.clone.1 | convolution fusion | flops 77853696 | bytes 5713920 | tf_op jit(solution)/shard_map/while/body/eval_jaxpr/qrhd,krhd->rhqk/dot_general | solution.py:36
  112.7 3.3 %fusion.58 = f32[4,8,32,96]{3,2,1,0:T(8,128)S(1)} fusion(bf16[384,4,8,32]{0,3,2,1:T(8,128)(2,1)S(1)} %bitcast.99, f32[4,8,96,384]{3,2,1,0:T(8,128)} %get-tuple-element.305), kind=kOutput, calls=%fused_computation.3.clone.1 | convolution fusion | flops 77856768 | bytes 5898240 | tf_op jit(solution)/shard_map/while/body/eval_jaxpr/rhqk,krhd->qrhd/dot_general | solution.py:42
  115.9 1.1 constant_dynamic-slice_fusion.10
  118.3 1.5 constant_dynamic-slice_fusion.9
  120.1 1.1 constant_dynamic-slice_fusion.8
  121.5 3.2 %fusion.56 = (f32[4,8,96]{2,1,0:T(8,128)S(1)}, f32[4,8,96,384]{3,2,1,0:T(8,128)}) fusion(bf16[96,4,8,32]{0,3,2,1:T(8,128)(2,1)S(1)} %bitcast.100, bf16[384,4,8,32]{0,3,2,1:T(8,128)(2,1)S(1)} %bitcast.98), kind=kOutput, calls=%fused_computation.2.clone.1 | convolution fusion | flops 77853696 | bytes 5713920 | tf_op jit(solution)/shard_map/while/body/eval_jaxpr/qrhd,krhd->rhqk/dot_general | solution.py:36
  125.0 3.3 %fusion.58 = f32[4,8,32,96]{3,2,1,0:T(8,128)S(1)} fusion(bf16[384,4,8,32]{0,3,2,1:T(8,128)(2,1)S(1)} %bitcast.99, f32[4,8,96,384]{3,2,1,0:T(8,128)} %get-tuple-element.305), kind=kOutput, calls=%fused_computation.3.clone.1 | convolution fusion | flops 77856768 | bytes 5898240 | tf_op jit(solution)/shard_map/while/body/eval_jaxpr/rhqk,krhd->qrhd/dot_general | solution.py:42
  128.3 1.0 constant_dynamic-slice_fusion.10
  130.6 1.5 constant_dynamic-slice_fusion.9
  132.4 1.1 constant_dynamic-slice_fusion.8
  133.8 3.2 %fusion.56 = (f32[4,8,96]{2,1,0:T(8,128)S(1)}, f32[4,8,96,384]{3,2,1,0:T(8,128)}) fusion(bf16[96,4,8,32]{0,3,2,1:T(8,128)(2,1)S(1)} %bitcast.100, bf16[384,4,8,32]{0,3,2,1:T(8,128)(2,1)S(1)} %bitcast.98), kind=kOutput, calls=%fused_computation.2.clone.1 | convolution fusion | flops 77853696 | bytes 5713920 | tf_op jit(solution)/shard_map/while/body/eval_jaxpr/qrhd,krhd->rhqk/dot_general | solution.py:36
  137.3 3.3 %fusion.58 = f32[4,8,32,96]{3,2,1,0:T(8,128)S(1)} fusion(bf16[384,4,8,32]{0,3,2,1:T(8,128)(2,1)S(1)} %bitcast.99, f32[4,8,96,384]{3,2,1,0:T(8,128)} %get-tuple-element.305), kind=kOutput, calls=%fused_computation.3.clone.1 | convolution fusion | flops 77856768 | bytes 5898240 | tf_op jit(solution)/shard_map/while/body/eval_jaxpr/rhqk,krhd->qrhd/dot_general | solution.py:42
  142.9 1.5 constant_dynamic-slice_fusion.9
  144.7 1.1 constant_dynamic-slice_fusion.8
  146.1 3.2 %fusion.56 = (f32[4,8,96]{2,1,0:T(8,128)S(1)}, f32[4,8,96,384]{3,2,1,0:T(8,128)}) fusion(bf16[96,4,8,32]{0,3,2,1:T(8,128)(2,1)S(1)} %bitcast.100, bf16[384,4,8,32]{0,3,2,1:T(8,128)(2,1)S(1)} %bitcast.98), kind=kOutput, calls=%fused_computation.2.clone.1 | convolution fusion | flops 77853696 | bytes 5713920 | tf_op jit(solution)/shard_map/while/body/eval_jaxpr/qrhd,krhd->rhqk/dot_general | solution.py:36
  149.6 3.3 %fusion.58 = f32[4,8,32,96]{3,2,1,0:T(8,128)S(1)} fusion(bf16[384,4,8,32]{0,3,2,1:T(8,128)(2,1)S(1)} %bitcast.99, f32[4,8,96,384]{3,2,1,0:T(8,128)} %get-tuple-element.305), kind=kOutput, calls=%fused_computation.3.clone.1 | convolution fusion | flops 77856768 | bytes 5898240 | tf_op jit(solution)/shard_map/while/body/eval_jaxpr/rhqk,krhd->qrhd/dot_general | solution.py:42
  152.8 1.0 constant_dynamic-slice_fusion.10
  155.2 1.5 constant_dynamic-slice_fusion.9
  157.0 1.1 constant_dynamic-slice_fusion.8
  158.3 3.2 %fusion.56 = (f32[4,8,96]{2,1,0:T(8,128)S(1)}, f32[4,8,96,384]{3,2,1,0:T(8,128)}) fusion(bf16[96,4,8,32]{0,3,2,1:T(8,128)(2,1)S(1)} %bitcast.100, bf16[384,4,8,32]{0,3,2,1:T(8,128)(2,1)S(1)} %bitcast.98), kind=kOutput, calls=%fused_computation.2.clone.1 | convolution fusion | flops 77853696 | bytes 5713920 | tf_op jit(solution)/shard_map/while/body/eval_jaxpr/qrhd,krhd->rhqk/dot_general | solution.py:36
  161.8 3.3 %fusion.58 = f32[4,8,32,96]{3,2,1,0:T(8,128)S(1)} fusion(bf16[384,4,8,32]{0,3,2,1:T(8,128)(2,1)S(1)} %bitcast.99, f32[4,8,96,384]{3,2,1,0:T(8,128)} %get-tuple-element.305), kind=kOutput, calls=%fused_computation.3.clone.1 | convolution fusion | flops 77856768 | bytes 5898240 | tf_op jit(solution)/shard_map/while/body/eval_jaxpr/rhqk,krhd->qrhd/dot_general | solution.py:42
  165.1 1.0 constant_dynamic-slice_fusion.10
  167.4 1.5 constant_dynamic-slice_fusion.9
  169.2 1.1 constant_dynamic-slice_fusion.8
  170.6 3.2 %fusion.56 = (f32[4,8,96]{2,1,0:T(8,128)S(1)}, f32[4,8,96,384]{3,2,1,0:T(8,128)}) fusion(bf16[96,4,8,32]{0,3,2,1:T(8,128)(2,1)S(1)} %bitcast.100, bf16[384,4,8,32]{0,3,2,1:T(8,128)(2,1)S(1)} %bitcast.98), kind=kOutput, calls=%fused_computation.2.clone.1 | convolution fusion | flops 77853696 | bytes 5713920 | tf_op jit(solution)/shard_map/while/body/eval_jaxpr/qrhd,krhd->rhqk/dot_general | solution.py:36
  174.1 3.3 %fusion.58 = f32[4,8,32,96]{3,2,1,0:T(8,128)S(1)} fusion(bf16[384,4,8,32]{0,3,2,1:T(8,128)(2,1)S(1)} %bitcast.99, f32[4,8,96,384]{3,2,1,0:T(8,128)} %get-tuple-element.305), kind=kOutput, calls=%fused_computation.3.clone.1 | convolution fusion | flops 77856768 | bytes 5898240 | tf_op jit(solution)/shard_map/while/body/eval_jaxpr/rhqk,krhd->qrhd/dot_general | solution.py:42
  179.6 2.2 div.23
  181.9 5.5 %copy.72 = f32[96,32,256]{2,0,1:T(8,128)} copy(f32[96,32,256]{0,2,1:T(8,128)} %bitcast.101) | data formatting | bytes 6291456 | tf_op jit(solution)/shard_map/div | solution.py:120
  187.3 4.2 %multiply_convert_fusion = bf16[96,32,256]{2,0,1:T(8,128)(2,1)S(1)} fusion(f32[96,32,256]{2,0,1:T(8,128)} %get-tuple-element.174, f32[96,32,256]{2,0,1:T(8,128)} %copy.72, bf16[96,32,256]{2,0,1:T(8,128)(2,1)S(1)} %copy-done.5, bf16[256,256]{1,0:T(8,128)(2,1)S(1)} %copy-done.9), kind=kOutput, calls=%fused_computation.36 | convolution fusion | flops 407371776 | bytes 9568256 | tf_op jit(solution)/shard_map/dot_general | solution.py:23
  191.6 2.3 convolution_convert_fusion.1
  193.9 68.8 %while.28 = (s32[]{:T(128)}, bf16[2,8,128,128]{3,2,1,0:T(8,128)(2,1)S(1)}, s32[2]{0:T(128)S(1)}, bf16[384,8192]{1,0:T(8,128)(2,1)}, bf16[384,256]{1,0:T(8,128)(2...) while((s32[]{:T(128)}, ...), condition=%wide.region_6.7_spmd, body=%wide.region_5.6_spmd.sunk | while | flops 1348599808 | bytes 51577028 | solution.py:98
  195.2 5.2 %fusion.64 = f32[256,4096]{0,1:T(8,128)} fusion(bf16[384,256]{1,0:T(8,128)(2,1)S(1)} %get-tuple-element.366, bf16[384,8192]{1,0:T(8,128)(2,1)} %get-tuple-element.365, s32[]{:T(128)S(6)} %select_n.25), kind=kOutput, calls=%fused_computation.15.clone.1 | convolution fusion | flops 806354944 | bytes 7536644 | tf_op jit(solution)/shard_map/while/body/eval_jaxpr/dot_general | solution.py:69
  200.4 10.9 %reshape.80 = f32[8,32,128,32]{1,0,3,2:T(8,128)} reshape(f32[256,4096]{0,1:T(8,128)} %fusion.64) | data formatting | bytes 8388608 | tf_op jit(solution)/shard_map/while/body/eval_jaxpr/reshape | solution.py:74
  211.3 12.7 %copy.113 = f32[8,32,128,32]{2,3,1,0:T(8,128)} copy(f32[8,32,128,32]{1,0,3,2:T(8,128)} %reshape.80) | data formatting | bytes 8388608 | tf_op jit(solution)/shard_map/while/body/eval_jaxpr/reshape | solution.py:74
  224.0 3.1 %convolution_bitcast_fusion.2 = f32[8,128,128]{2,1,0:T(8,128)S(1)} fusion(f32[8,32,128,32]{2,3,1,0:T(8,128)} %copy.113, bf16[32,32,128]{2,1,0:T(8,128)(2,1)S(1)} %get-tuple-element.367), kind=kOutput, calls=%fused_computation.19.clone.1 | convolution fusion | flops 269484032 | bytes 4980736 | tf_op jit(solution)/shard_map/while/body/eval_jaxpr/icje,cep->ijp/dot_general | solution.py:77
  229.5 5.2 %fusion.64 = f32[256,4096]{0,1:T(8,128)} fusion(bf16[384,256]{1,0:T(8,128)(2,1)S(1)} %get-tuple-element.366, bf16[384,8192]{1,0:T(8,128)(2,1)} %get-tuple-element.365, s32[]{:T(128)S(6)} %select_n.25), kind=kOutput, calls=%fused_computation.15.clone.1 | convolution fusion | flops 806354944 | bytes 7536644 | tf_op jit(solution)/shard_map/while/body/eval_jaxpr/dot_general | solution.py:69
  234.8 10.9 %reshape.80 = f32[8,32,128,32]{1,0,3,2:T(8,128)} reshape(f32[256,4096]{0,1:T(8,128)} %fusion.64) | data formatting | bytes 8388608 | tf_op jit(solution)/shard_map/while/body/eval_jaxpr/reshape | solution.py:74
  245.7 12.7 %copy.113 = f32[8,32,128,32]{2,3,1,0:T(8,128)} copy(f32[8,32,128,32]{1,0,3,2:T(8,128)} %reshape.80) | data formatting | bytes 8388608 | tf_op jit(solution)/shard_map/while/body/eval_jaxpr/reshape | solution.py:74
  258.4 3.1 %convolution_bitcast_fusion.2 = f32[8,128,128]{2,1,0:T(8,128)S(1)} fusion(f32[8,32,128,32]{2,3,1,0:T(8,128)} %copy.113, bf16[32,32,128]{2,1,0:T(8,128)(2,1)S(1)} %get-tuple-element.367), kind=kOutput, calls=%fused_computation.19.clone.1 | convolution fusion | flops 269484032 | bytes 4980736 | tf_op jit(solution)/shard_map/while/body/eval_jaxpr/icje,cep->ijp/dot_general | solution.py:77
  (109 shorter events, 25.5 us)
Async XLA Ops:
  7.2 63.0 %copy-start = (bf16[256,512]{1,0:T(8,128)(2,1)S(1)}, bf16[256,512]{1,0:T(8,128)(2,1)}, u32[]{:S(2)}) copy-start(bf16[256,512]{1,0:T(8,128)(2,1)} %param.13) | copy-start | bytes 786436
  7.2 5.5 %copy-start.3 = (bf16[96,32,256]{2,1,0:T(8,128)(2,1)S(1)}, bf16[96,32,256]{2,1,0:T(8,128)(2,1)}, u32[]{:S(2)}) copy-start(bf16[96,32,256]{2,1,0:T(8,128)(2,1)} %param.11) | copy-start | bytes 4718596
  7.2 63.0 %all-gather.3.cloned.1.call-start = ((), (), s32[]{:S(2)}) async-start(), calls=%async_computation | async-start | bytes 7864320 | tf_op jit(solution)/shard_map/all_gather | solution.py:115
  9.7 6.1 %copy-start.10 = (bf16[256,64]{0,1:T(8,128)(2,1)S(1)}, bf16[256,64]{0,1:T(8,128)(2,1)}, u32[]{:S(2)}) copy-start(bf16[256,64]{0,1:T(8,128)(2,1)} %param.16) | copy-start | bytes 98308
  15.8 178.1 %all-gather.5.cloned.1.call-start = ((), (), s32[]{:S(2)}) async-start(), calls=%async_computation.1 | async-start | bytes 7077888 | tf_op jit(solution)/shard_map/all_gather | solution.py:140
  18.4 14.6 %copy-start.4 = (bf16[96,32,256]{2,0,1:T(8,128)(2,1)S(1)}, bf16[96,32,256]{2,0,1:T(8,128)(2,1)}, u32[]{:S(2)}) copy-start(bf16[96,32,256]{2,0,1:T(8,128)(2,1)} %fusion.22) | copy-start | bytes 4718596
  18.4 14.6 %copy-start.6 = (bf16[256,256]{1,0:T(8,128)(2,1)S(1)}, bf16[256,256]{1,0:T(8,128)(2,1)}, u32[]{:S(2)}) copy-start(bf16[256,256]{1,0:T(8,128)(2,1)} %param.12) | copy-start | bytes 393220
  181.9 5.5 %copy-start.5 = (bf16[96,32,256]{2,0,1:T(8,128)(2,1)S(1)}, bf16[96,32,256]{2,0,1:T(8,128)(2,1)}, u32[]{:S(2)}) copy-start(bf16[96,32,256]{2,0,1:T(8,128)(2,1)} %fusion.22) | copy-start | bytes 4718596
  181.9 5.5 %copy-start.9 = (bf16[256,256]{1,0:T(8,128)(2,1)S(1)}, bf16[256,256]{1,0:T(8,128)(2,1)}, u32[]{:S(2)}) copy-start(bf16[256,256]{1,0:T(8,128)(2,1)} %param.14) | copy-start | bytes 393220
  187.3 4.2 %copy-start.7 = (bf16[256,256]{1,0:T(8,128)(2,1)S(1)}, bf16[256,256]{1,0:T(8,128)(2,1)}, u32[]{:S(2)}) copy-start(bf16[256,256]{1,0:T(8,128)(2,1)} %param.15) | copy-start | bytes 393220
  191.6 2.3 copy-start.8
  224.0 3.4 %copy-start.2 = (f32[8,32,128,32]{2,3,1,0:T(8,128)S(1)}, f32[8,32,128,32]{2,3,1,0:T(8,128)}, u32[]{:S(2)}) copy-start(f32[8,32,128,32]{2,3,1,0:T(8,128)} %copy.113) | copy-start | bytes 12582916 | tf_op jit(solution)/shard_map/while
  258.4 3.4 %copy-start.2 = (f32[8,32,128,32]{2,3,1,0:T(8,128)S(1)}, f32[8,32,128,32]{2,3,1,0:T(8,128)}, u32[]{:S(2)}) copy-start(f32[8,32,128,32]{2,3,1,0:T(8,128)} %copy.113) | copy-start | bytes 12582916 | tf_op jit(solution)/shard_map/while
  262.7 1.0 copy-start.1
Sparse Core Ops, SparseCore 0:
  15.9 54.1 all-gather.2
  72.3 99.5 all-gather.4
where the time goes:
time: 273 us; the launch traced here: 270 us
  local copies, waits for them, and re-layouts  110 us (40%)
  matrix products  90.2 us (33%)
  blocking collectives  26.3 us (10%)
  waiting for transfers between devices  19.2 us (7%)
  between operations  14.2 us (5%)
  other arithmetic  8.96 us (3%)
    reshape x4, local copies, waits for them, and re-layouts, outer_panel(): products = products.reshape(row_count, factor, column_total, factor)  47.2 us
    dot_general x8, matrix products, attend_group(): jnp.einsum('rhqk,krhd->qrhd', weights, head_values, preferred_element_typ...  26.2 us
    dot_general x8, matrix products, attend_group(): jnp.einsum('qrhd,krhd->rhqk', per_head_query, head_keys, preferred_elemen...  25.2 us
    dot_general x5, matrix products, apply_projection(): return jnp.dot(normed, weight, preferred_element_type=jnp.float32)  20.5 us
    all_gather x1, waiting for transfers between devices, per_device(): lax.all_gather(normed, 'seq', axis=0, tiled=True)  19.1 us
    all_gather x1, blocking collectives, per_device(): lax.all_gather(left_factor, 'seq', axis=0, tiled=True)  14.7 us
    slice x8, local copies, waits for them, and re-layouts, attend_group(): keyval_slice[:, :, hidden:].reshape(key_count, group_size, HEADS, HC)  11.8 us
    all_gather x1, blocking collectives, per_device(): lax.all_gather(right_factor, 'seq', axis=0, tiled=True)  11.6 us
  transfers between devices with their start and end apart: 2, of which 1 were waited for; matrix products, arithmetic and copies ran while one was open for 49% of the time, Pallas kernels for 0%

commit v1 on v0

v1 whole, which is shorter than its diff:
```python
import math

import jax
import jax.numpy as jnp
from jax import lax
from jax.experimental import pallas as pl
from jax.experimental.pallas import tpu as pltpu
from jax.sharding import PartitionSpec as P

HEADS = 8
HC = 32
LOG2E = 1.4426950408889634
epsilon = 1e-05
NT = (((1,), (1,)), ((), ()))


def mm(a, b):
    return jnp.dot(a, b, preferred_element_type=jnp.float32)


def mm_nt(a, b):
    return lax.dot_general(a, b, NT, preferred_element_type=jnp.float32)


def normalize_kernel(x_ref, o_ref, scratch):
    seqs, residues, width = x_ref.shape
    step = 8

    def norm(i, carry):
        values = x_ref[pl.ds(i * step, step)].reshape(step * residues, width).astype(jnp.float32)
        centered = values - jnp.mean(values, axis=-1, keepdims=True)
        spread = jnp.mean(centered * centered, axis=-1, keepdims=True)
        normed = centered * lax.rsqrt(spread + epsilon)
        for part in range(width // 128):
            scratch[part, pl.ds(i * (step * residues), step * residues), :] = normed[
                :, part * 128 : (part + 1) * 128
            ]
        return carry

    lax.fori_loop(0, seqs // step, norm, 0)

    def move(r, carry):
        for part in range(width // 128):
            o_ref[r, :, part * 128 : (part + 1) * 128] = scratch[
                part, pl.ds(r, seqs, residues), :
            ].astype(jnp.bfloat16)
        return carry

    lax.fori_loop(0, residues, move, 0)


def attend_residues(own, everything, wqg, wkv, wout):
    groups, count, seqs, width = everything.shape
    hidden = HEADS * HC
    kv = mm(everything.reshape(groups * count * seqs, width), wkv).astype(jnp.bfloat16)
    kv = kv.reshape(groups, count, seqs, 2 * hidden)
    qg = mm(own.reshape(count * seqs, width), wqg)
    queries = qg[:, :hidden].astype(jnp.bfloat16)
    gating = jax.nn.sigmoid(qg[:, hidden:])
    head_of = lax.broadcasted_iota(jnp.int32, (seqs, hidden), 1) // HC
    gated = []
    for n in range(count):
        q = queries[n * seqs : (n + 1) * seqs].astype(jnp.float32)
        stacked = jnp.concatenate(
            [jnp.where(head_of == h, q, 0.0).astype(jnp.bfloat16) for h in range(HEADS)], axis=0
        )
        keys = kv[:, n, :, :hidden].reshape(groups * seqs, hidden)
        values = kv[:, n, :, hidden:].reshape(groups * seqs, hidden)
        exponent = jnp.exp2(mm_nt(stacked, keys) * (LOG2E / math.sqrt(HC)))
        inverse = 1.0 / jnp.sum(exponent, axis=-1, keepdims=True)
        weighted = mm(exponent.astype(jnp.bfloat16), values)
        attended = jnp.zeros((seqs, hidden), jnp.float32)
        for h in range(HEADS):
            rows = slice(h * seqs, (h + 1) * seqs)
            attended = jnp.where(head_of == h, weighted[rows] * inverse[rows], attended)
        gated.append((gating[n * seqs : (n + 1) * seqs] * attended).astype(jnp.bfloat16))
    return mm(jnp.concatenate(gated, axis=0), wout)


def attention_kernel(own_ref, all_ref, wqg_ref, wkv_ref, wout_ref, o_ref, scratch):
    step = pl.program_id(0)
    count, seqs, width = own_ref.shape
    residues = o_ref.shape[1]
    update = attend_residues(
        own_ref[...], all_ref[...], wqg_ref[...], wkv_ref[...], wout_ref[...]
    )
    for n in range(count):
        for part in range(width // 128):
            scratch[part, pl.ds(step * count + n, seqs, residues), :] = update[
                n * seqs : (n + 1) * seqs, part * 128 : (part + 1) * 128
            ]

    @pl.when(step == pl.num_programs(0) - 1)
    def _():
        chunk = 8

        def finish(i, carry):
            for part in range(width // 128):
                o_ref[pl.ds(i * chunk, chunk), :, part * 128 : (part + 1) * 128] = (
                    scratch[part, pl.ds(i * (chunk * residues), chunk * residues), :]
                    .astype(jnp.bfloat16)
                    .reshape(chunk, residues, 128)
                )
            return carry

        lax.fori_loop(0, seqs // chunk, finish, 0)


def factor_kernel(all_ref, wft_ref, left_ref, right_ref, scratch):
    step = pl.program_id(0)
    groups, count, seqs, width = all_ref.shape
    factor = wft_ref.shape[0] // 2
    residues = right_ref.shape[1]
    for n in range(count):
        both = mm_nt(wft_ref[...], all_ref[:, n].reshape(groups * seqs, width))
        left_ref[n] = both[:factor].astype(jnp.bfloat16)
        for part in range(groups * seqs // 128):
            scratch[part, pl.ds(step * count + n, factor, residues), :] = both[
                factor:, part * 128 : (part + 1) * 128
            ]

    @pl.when(step == pl.num_programs(0) - 1)
    def _():
        for part in range(groups * seqs // 128):
            right_ref[:, :, part * 128 : (part + 1) * 128] = (
                scratch[part].astype(jnp.bfloat16).reshape(factor, residues, 128)
            )


def pair_kernel(scaling, left_ref, right_ref, w_ref, o_ref, scratch):
    blocks, factor, residues, depth = right_ref.shape
    rows = o_ref.shape[0]
    channels = o_ref.shape[2]
    lanes = left_ref.shape[0]
    pack = 128 // factor
    span = blocks * residues
    for b in range(blocks):
        products = (
            mm_nt(right_ref[b].reshape(factor * residues, depth), left_ref[...]) * scaling
        ).astype(jnp.bfloat16)
        for e in range(factor):
            for g in range(lanes // 128):
                scratch[pl.ds(g * span + b * residues, residues), e * 128 : (e + 1) * 128] = (
                    products[e * residues : (e + 1) * residues, g * 128 : (g + 1) * 128]
                )
    pair = mm(scratch[...], w_ref[...])
    for i in range(rows):
        g, k = i // pack, i % pack
        o_ref[i] = pair[g * span : (g + 1) * span, k * channels : (k + 1) * channels].astype(
            jnp.bfloat16
        )


def whole(*shape):
    return pl.BlockSpec(shape, lambda i: (0,) * len(shape))


LIMIT = pltpu.CompilerParams(vmem_limit_bytes=60 * 1024 * 1024)


def per_device(alignment, query_weight, w_keyval, w_gate, output_weight, w_factors, w_pair_out):
    seqs, residues, width = alignment.shape
    groups = lax.axis_size("seq")
    blocks = lax.axis_size("res")
    depth = seqs * groups
    factor = w_factors.shape[1] // 2
    channels = w_pair_out.shape[1]
    hidden = query_weight.shape[1]
    own_rows = residues // groups

    normed = pl.pallas_call(
        normalize_kernel,
        out_shape=jax.ShapeDtypeStruct((residues, seqs, width), jnp.bfloat16),
        scratch_shapes=[pltpu.VMEM((width // 128, seqs * residues, 128), jnp.float32)],
        compiler_params=LIMIT,
        name="normalize",
    )(alignment)
    everything = lax.all_gather(normed, "seq", axis=0, tiled=False)

    count = 4
    wft = jnp.transpose(w_factors)
    left, right = pl.pallas_call(
        factor_kernel,
        grid=(residues // count,),
        in_specs=[
            pl.BlockSpec((groups, count, seqs, width), lambda i: (0, i, 0, 0)),
            whole(2 * factor, width),
        ],
        out_specs=[
            pl.BlockSpec((count, factor, depth), lambda i: (i, 0, 0)),
            whole(factor, residues, depth),
        ],
        out_shape=[
            jax.ShapeDtypeStruct((residues, factor, depth), jnp.bfloat16),
            jax.ShapeDtypeStruct((factor, residues, depth), jnp.bfloat16),
        ],
        scratch_shapes=[pltpu.VMEM((depth // 128, factor * residues, 128), jnp.float32)],
        compiler_params=LIMIT,
        name="factors",
    )(everything, wft)
    right_all = lax.all_gather(right, "res", axis=0, tiled=False)

    wqg = jnp.concatenate([query_weight, w_gate], axis=1)
    alignment_update = pl.pallas_call(
        attention_kernel,
        grid=(residues // count,),
        in_specs=[
            pl.BlockSpec((count, seqs, width), lambda i: (i, 0, 0)),
            pl.BlockSpec((groups, count, seqs, width), lambda i: (0, i, 0, 0)),
            whole(width, 2 * hidden),
            whole(width, 2 * hidden),
            whole(hidden, width),
        ],
        out_specs=whole(seqs, residues, width),
        out_shape=jax.ShapeDtypeStruct((seqs, residues, width), jnp.bfloat16),
        scratch_shapes=[pltpu.VMEM((width // 128, seqs * residues, 128), jnp.float32)],
        compiler_params=LIMIT,
        cost_estimate=pl.CostEstimate(
            flops=30_000_000_000, bytes_accessed=10_000_000, transcendentals=10_000_000
        ),
        name="attention",
    )(normed, everything, wqg, w_keyval, output_weight)

    pack = 128 // factor
    w = jnp.transpose(w_pair_out.reshape(factor, factor, channels), (1, 0, 2))
    eye = jnp.eye(pack, dtype=w.dtype)
    spread = (w[:, None, :, None, :] * eye[None, :, None, :, None]).reshape(
        factor * pack * factor, pack * channels
    )
    own_left = lax.dynamic_slice_in_dim(
        left, lax.axis_index("seq") * own_rows, own_rows, 0
    ).reshape(own_rows * factor, depth)
    each = math.gcd(blocks, 4)
    pair = pl.pallas_call(
        lambda *refs: pair_kernel(1.0 / depth, *refs),
        grid=(blocks // each,),
        in_specs=[
            whole(own_rows * factor, depth),
            pl.BlockSpec((each, factor, residues, depth), lambda i: (i, 0, 0, 0)),
            whole(*spread.shape),
        ],
        out_specs=pl.BlockSpec((own_rows, each * residues, channels), lambda i: (0, i, 0)),
        out_shape=jax.ShapeDtypeStruct((own_rows, blocks * residues, channels), jnp.bfloat16),
        scratch_shapes=[
            pltpu.VMEM((own_rows // pack * each * residues, factor * 128), jnp.bfloat16)
        ],
        compiler_params=LIMIT,
        name="pair",
    )(own_left, right_all, spread)
    return (alignment_update, pair)


def solution(mesh):
    in_specs = (P("seq", "res", None), P(), P(), P(), P(), P(), P())
    out_specs = (P("seq", "res", None), P(("res", "seq"), None, None))
    return jax.shard_map(
        per_device, mesh=mesh, in_specs=in_specs, out_specs=out_specs, check_vma=False
    )
```

time: 273 us -> 188 us (0.69)
  local copies, waits for them, and re-layouts: 110 us -> 4.4 us
  waiting for transfers between devices: 19.2 us -> 116 us
  matrix products: 90.2 us -> 0 us
  Pallas kernels: 0 us -> 51.1 us
  blocking collectives: 26.3 us -> 0 us
  other arithmetic: 8.96 us -> 2.38 us
    all_gather x2, waiting for transfers between devices: 19.1 us -> 116 us  [the longest x1 66.4 us: per_device(): right_all = lax.all_gather(right, 'res', axis=0, tiled=False)]
    dot_general x27 -> x0, matrix products: 90.2 us -> none  [the longest x8 26.2 us: attend_group(): jnp.einsum('rhqk,krhd->qrhd', weights, head_values, preferred_element_typ...]
    pallas_call x0 -> x4, Pallas kernels: none -> 51.1 us  [the longest x1 25.6 us: per_device(): pl.pallas_call(attention_kernel, grid=(residues // count,), in_specs=[pl....]
    reshape x6 -> x0, local copies, waits for them, and re-layouts: 48.4 us -> none  [the longest x4 47.2 us: outer_panel(): products = products.reshape(row_count, factor, column_total, factor)]
    all_gather x2 -> x0, blocking collectives: 26.3 us -> none  [the longest x1 14.7 us: per_device(): lax.all_gather(left_factor, 'seq', axis=0, tiled=True)]
    dynamic_slice x35 -> x1, local copies, waits for them, and re-layouts: 21.7 us -> 1.62 us  [per_device(): lax.dynamic_slice_in_dim(left, lax.axis_index('seq') * own_rows, own_rows...]
    slice x11 -> x0, local copies, waits for them, and re-layouts: 14.5 us -> none  [the longest x8 11.8 us: attend_group(): keyval_slice[:, :, hidden:].reshape(key_count, group_size, HEADS, HC)]
    dynamic_update_slice x16 -> x0, local copies, waits for them, and re-layouts: 7.93 us -> none  [attend_group(): lax.dynamic_update_slice_in_dim(accumulated, prior_values + weighted, sta...]
  transfers between devices with their start and end apart: 2 -> 2, of which waited for: 1 -> 2; matrix products, arithmetic and copies ran while one was open for 49% -> 4% of each run, Pallas kernels for 0% -> 14%
where the time goes in v1:
time: 188 us
  waiting for transfers between devices  116 us (62%)
  Pallas kernels  51.1 us (27%)
  between operations  14.1 us (8%)
  local copies, waits for them, and re-layouts  4.4 us (2%)
  other arithmetic  2.38 us (1%)
    all_gather x1, waiting for transfers between devices, per_device(): right_all = lax.all_gather(right, 'res', axis=0, tiled=False)  66.4 us
    all_gather x1, waiting for transfers between devices, per_device(): everything = lax.all_gather(normed, 'seq', axis=0, tiled=False)  49.2 us
    pallas_call x1, Pallas kernels, per_device(): pl.pallas_call(attention_kernel, grid=(residues // count,), in_specs=[pl....  25.6 us
    pallas_call x1, Pallas kernels, per_device(): pl.pallas_call(lambda *refs: pair_kernel(1.0 / depth, *refs), grid=(block...  8.85 us
    pallas_call x1, Pallas kernels, per_device(): pl.pallas_call(normalize_kernel, out_shape=jax.ShapeDtypeStruct((residues...  8.41 us
    pallas_call x1, Pallas kernels, per_device(): pl.pallas_call(factor_kernel, grid=(residues // count,), in_specs=[pl.Blo...  8.24 us
  transfers between devices with their start and end apart: 2, of which 2 were waited for; matrix products, arithmetic and copies ran while one was open for 4% of the time, Pallas kernels for 14%

profile of v1, /device:TPU:0, one launch (start us, length us, event | category | flops | bytes accessed | tf_op | source)
XLA Modules:
  0.0 187.7 jit_solution(4284697660899326664)
XLA Ops:
  7.2 0.0 all-gather.5.cloned.1.call-start
  7.2 8.4 %normalize.1.own_ref = bf16[32,96,256]{2,1,0:T(8,128)(2,1)} custom-call(bf16[96,32,256]{2,1,0:T(8,128)(2,1)} %x_ref.1), custom_call_target="tpu_custom_call" | custom-call | tf_op jit(solution)/shard_map/normalize/pallas_call | solution.py:171
  15.6 0.0 copy-start
  15.6 0.0 all-gather.5.cloned.1.call-update
  15.6 0.0 all-gather.7.cloned.1.call-start
  15.7 49.2 %all-gather.5.cloned.1.call-done = bf16[128,96,256]{2,1,0:T(8,128)(2,1)} async-done(((bf16[32,96,256]{2,1,0:T(8,128)(2,1)}), bf16[128,96,256]{2,1,0:T(8,128)(2,1)}) %all-gather.5.cloned.1.call-update) | async-done | bytes 6291472 | tf_op jit(solution)/shard_map/all_gather | solution.py:178
  64.9 8.2 %factors.1 = (bf16[32,32,384]{2,1,0:T(8,128)(2,1)}, bf16[32,32,384]{2,1,0:T(8,128)(2,1)}) custom-call(bf16[4,32,96,256]{3,2,1,0:T(8,128)(2,1)} %bitcast.14, bf16[64,256]{1,0:T(8,128)(2,1)} %bitcast.19), custom_call_target="tpu_custom_call" | custom-call | tf_op jit(solution)/shard_map/factors/pallas_call | solution.py:182
  73.1 0.0 all-gather.7.cloned.1.call-update
  73.2 0.0 copy-done
  73.2 0.1 copy.10
  73.3 1.6 broadcast_multiply_fusion
  74.9 0.0 copy-start.1
  75.0 0.0 copy-start.2
  75.0 2.6 %copy.13 = bf16[512,8,4,128]{3,1,2,0:T(8,128)(2,1)} copy(bf16[512,8,4,128]{3,2,1,0:T(4,128)(2,1)S(1)} %bitcast.13) | data formatting | bytes 8388608
  77.6 0.0 copy-done.1
  77.6 0.0 copy-done.2
  77.6 0.7 pad_maximum_fusion.wqg_ref
  78.3 1.6 constant_dynamic-slice_fusion
  80.0 25.6 %attention.1 = bf16[96,32,256]{2,1,0:T(8,128)(2,1)} custom-call(bf16[32,96,256]{2,1,0:T(8,128)(2,1)} %normalize.1.own_ref, bf16[4,32,96,256]{3,2,1,0:T(8,128)(2,1)} %bitcast.15, bf16[256,512]{1,0:T(8,128)(2,1)} %pad_maximum_fusion.wqg_ref, bf16[256,512]{1,0:T(8,128)(2,1)} %wkv_ref.1, bf16[256,256]{1,0:T(8,128)(2,1)} %wout_ref.1), custom_call_target="tpu_custom_call" | custom-call | flops 30000001024 | bytes 10000000 | tf_op jit(solution)/shard_map/attention/pallas_call | solution.py:204
  105.6 66.4 %all-gather.7.cloned.1.call-done = bf16[256,32,384]{2,1,0:T(8,128)(2,1)} async-done(((bf16[32,32,384]{2,1,0:T(8,128)(2,1)}), bf16[256,32,384]{2,1,0:T(8,128)(2,1)}) %all-gather.7.cloned.1.call-update) | async-done | bytes 6291472 | tf_op jit(solution)/shard_map/all_gather | solution.py:201
  172.0 8.8 %pair.1 = bf16[8,256,128]{2,1,0:T(8,128)(2,1)} custom-call(bf16[256,384]{1,0:T(8,128)(2,1)} %bitcast.17, bf16[8,32,32,384]{3,2,1,0:T(8,128)(2,1)} %bitcast.16, bf16[4096,512]{1,0:T(8,128)(2,1)} %bitcast.12), custom_call_target="tpu_custom_call" | custom-call | tf_op jit(solution)/shard_map/pair/pallas_call | solution.py:234
  (1 shorter events, 0.0 us)
Async XLA Ops:
  7.2 57.7 %all-gather.5.cloned.1.call-start = ((), (), s32[]{:S(2)}) async-start(), calls=%async_computation | async-start | bytes 7864320 | tf_op jit(solution)/shard_map/all_gather | solution.py:178
  15.6 57.5 %copy-start = (bf16[1024,128]{1,0:T(8,128)(2,1)S(1)}, bf16[1024,128]{1,0:T(8,128)(2,1)}, u32[]{:S(2)}) copy-start(bf16[1024,128]{1,0:T(8,128)(2,1)} %param.13) | copy-start | bytes 786436
  15.6 156.4 %all-gather.7.cloned.1.call-start = ((), (), s32[]{:S(2)}) async-start(), calls=%async_computation.1 | async-start | bytes 7077888 | tf_op jit(solution)/shard_map/all_gather | solution.py:201
  74.9 2.7 %copy-start.1 = (bf16[256,256]{1,0:T(8,128)(2,1)S(1)}, bf16[256,256]{1,0:T(8,128)(2,1)}, u32[]{:S(2)}) copy-start(bf16[256,256]{1,0:T(8,128)(2,1)} %param.10) | copy-start | bytes 393220
  75.0 2.7 %copy-start.2 = (bf16[256,256]{1,0:T(8,128)(2,1)S(1)}, bf16[256,256]{1,0:T(8,128)(2,1)}, u32[]{:S(2)}) copy-start(bf16[256,256]{1,0:T(8,128)(2,1)} %param.8) | copy-start | bytes 393220
Sparse Core Ops, SparseCore 0:
  15.8 49.0 all-gather.4
  73.3 98.6 all-gather.6

commit v2 on v1

v2 whole, which is shorter than its diff:
```python
import functools
import math

import jax
import jax.numpy as jnp
from jax import lax
from jax.experimental import pallas as pl
from jax.experimental.pallas import tpu as pltpu
from jax.sharding import PartitionSpec as P

HEADS = 8
HC = 32
LOG2E = 1.4426950408889634
epsilon = 1e-05
NT = (((1,), (1,)), ((), ()))


def mm(a, b):
    return jnp.dot(a, b, preferred_element_type=jnp.float32)


def mm_nt(a, b):
    return lax.dot_general(a, b, NT, preferred_element_type=jnp.float32)


MESH = pl.DeviceIdType.MESH
COUNT = 4


def attend_residues(own, everything, wqg, wkv, wout):
    groups, count, seqs, width = everything.shape
    hidden = HEADS * HC
    kv = mm(everything.reshape(groups * count * seqs, width), wkv).astype(jnp.bfloat16)
    kv = kv.reshape(groups, count, seqs, 2 * hidden)
    qg = mm(own.reshape(count * seqs, width), wqg)
    queries = qg[:, :hidden].astype(jnp.bfloat16)
    gating = jax.nn.sigmoid(qg[:, hidden:])
    head_of = lax.broadcasted_iota(jnp.int32, (seqs, hidden), 1) // HC
    gated = []
    for n in range(count):
        q = queries[n * seqs : (n + 1) * seqs].astype(jnp.float32)
        stacked = jnp.concatenate(
            [jnp.where(head_of == h, q, 0.0).astype(jnp.bfloat16) for h in range(HEADS)], axis=0
        )
        keys = kv[:, n, :, :hidden].reshape(groups * seqs, hidden)
        values = kv[:, n, :, hidden:].reshape(groups * seqs, hidden)
        exponent = jnp.exp2(mm_nt(stacked, keys) * (LOG2E / math.sqrt(HC)))
        inverse = 1.0 / jnp.sum(exponent, axis=-1, keepdims=True)
        weighted = mm(exponent.astype(jnp.bfloat16), values)
        attended = jnp.zeros((seqs, hidden), jnp.float32)
        for h in range(HEADS):
            rows = slice(h * seqs, (h + 1) * seqs)
            attended = jnp.where(head_of == h, weighted[rows] * inverse[rows], attended)
        gated.append((gating[n * seqs : (n + 1) * seqs] * attended).astype(jnp.bfloat16))
    return mm(jnp.concatenate(gated, axis=0), wout)


def block_kernel(
    scaling,
    blocks,
    groups,
    x_ref,
    wqg_ref,
    wkv_ref,
    wout_ref,
    wft_ref,
    wpair_ref,
    o_ref,
    pair_ref,
    gathered,
    strided,
    factor_rows,
    left_all,
    right_all,
    outer,
    outgoing,
    incoming,
    cross_send,
    cross_recv,
    twin_send,
    twin_recv,
    relay_send,
    relay_recv,
    ring_send,
    ring_recv,
    share_send,
    share_recv,
    swap_send,
    swap_recv,
):
    seqs, residues, width = x_ref.shape
    depth = seqs * groups
    factor = wft_ref.shape[0] // 2
    own_rows = residues // groups
    channels = pair_ref.shape[2]
    half = residues // 2
    parts = residues // COUNT
    half_parts = parts // 2
    hops = blocks // 2
    r = lax.axis_index("res")
    q = lax.axis_index("seq")
    core = lax.rem(q, 2)
    side = q // 2
    twin = q + 1 - 2 * core
    across = lax.rem(q + 2, groups)
    twin_across = lax.rem(twin + 2, groups)

    def ring_of(block):
        z, y = block // 2, lax.rem(block, 2)
        return jnp.where(y == 0, z, blocks - 1 - z)

    def block_of(place):
        return jnp.where(place < blocks // 2, 2 * place, 2 * (blocks - 1 - place) + 1)

    place = ring_of(r)
    ahead = block_of(lax.rem(place + 1, blocks))
    behind = block_of(lax.rem(place + blocks - 1, blocks))

    barrier = pltpu.get_barrier_semaphore()
    for target in ((r, twin), (r, across), (ahead, q), (behind, q)):
        pl.semaphore_signal(barrier, inc=1, device_id=target, device_id_type=MESH)
    pl.semaphore_wait(barrier, 4)

    def part_at(p):
        return lax.rem(p + side * half_parts, parts)

    def rows_of(owner, part):
        return gathered.at[owner, pl.ds(part * COUNT, COUNT)]

    def send(ref, dst, send_sem, recv_sem, target):
        return pltpu.make_async_remote_copy(
            src_ref=ref,
            dst_ref=dst,
            send_sem=send_sem,
            recv_sem=recv_sem,
            device_id=target,
            device_id_type=MESH,
        )

    def cross(owner, p, part):
        block = rows_of(owner, part)
        return send(block, block, cross_send.at[p], cross_recv.at[p], (r, across))

    def direct(owner, p, part):
        block = rows_of(owner, part)
        return send(block, block, twin_send.at[p], twin_recv.at[p], (r, twin))

    def relay(owner, p, part):
        block = rows_of(owner, part)
        return send(block, block, relay_send.at[p], relay_recv.at[p], (r, twin))

    step = 8
    for turn in range(2):
        which = (1 - side) if turn == 0 else side
        base = pl.multiple_of(which * half, half)

        def norm(i, carry):
            values = (
                x_ref[pl.ds(i * step, step), pl.ds(base, half), :]
                .reshape(step * half, width)
                .astype(jnp.float32)
            )
            centered = values - jnp.mean(values, axis=-1, keepdims=True)
            spread = jnp.mean(centered * centered, axis=-1, keepdims=True)
            normed = centered * lax.rsqrt(spread + epsilon)
            for part in range(width // 128):
                strided[part, pl.ds(i * (step * half), step * half), :] = normed[
                    :, part * 128 : (part + 1) * 128
                ]
            return carry

        lax.fori_loop(0, seqs // step, norm, 0)

        def move(k, carry):
            for n in range(COUNT):
                for part in range(width // 128):
                    gathered[q, base + k * COUNT + n, :, part * 128 : (part + 1) * 128] = strided[
                        part, pl.ds(k * COUNT + n, seqs, half), :
                    ].astype(jnp.bfloat16)
            return carry

        def start_across(k, carry):
            cross(q, turn * half_parts + k, which * half_parts + k).start()
            return carry

        def move_and_start(k, carry):
            move(k, carry)
            return start_across(k, carry)

        lax.fori_loop(0, half_parts, move_and_start, 0)

    def start_twin(p, carry):
        direct(q, p, part_at(p)).start()
        return carry

    lax.fori_loop(0, parts, start_twin, 0)

    own_e = pl.ds(pl.multiple_of(core * (factor // 2), factor // 2), factor // 2)
    twin_e = pl.ds(pl.multiple_of((1 - core) * (factor // 2), factor // 2), factor // 2)

    def ring_copy(way, hop):
        shift = blocks - hop if way == 0 else hop
        block = block_of(lax.rem(place + shift, blocks))
        ref = right_all.at[block, own_e]
        return send(
            ref,
            ref,
            ring_send.at[way, hop],
            ring_recv.at[way, hop],
            ((ahead if way == 0 else behind), q),
        )

    def landed(way, hop):
        shift = blocks - hop - 1 if way == 0 else hop + 1
        return block_of(lax.rem(place + shift, blocks))

    def share_copy(way, hop, mine=True):
        ref = right_all.at[landed(way, hop), own_e if mine else twin_e]
        return send(ref, ref, share_send.at[way, hop], share_recv.at[way, hop], (r, twin))

    def arrive(way, hop):
        block = landed(way, hop)
        ref = right_all.at[block, own_e]
        send(
            ref, ref, ring_send.at[way, hop], ring_recv.at[way, hop], ((ahead if way == 0 else behind), q)
        ).wait_recv()

    ways = (hops, blocks - 1 - hops)

    def advance(hop):
        for way in range(2):

            @pl.when(hop <= ways[way])
            def _():
                @pl.when(hop > 0)
                def _():
                    arrive(way, hop - 1)

                @pl.when(hop < ways[way])
                def _():
                    ring_copy(way, hop).start()

                @pl.when(hop > 0)
                def _():
                    share_copy(way, hop - 1).start()

    def one_part(p, carry):
        part = part_at(p)
        cross(across, p, part).wait_recv()
        relay(across, p, part).start()
        direct(twin, p, part).wait_recv()
        relay(twin_across, p, part).wait_recv()
        everything = gathered[:, pl.ds(part * COUNT, COUNT)]
        for n in range(COUNT):
            both = mm_nt(wft_ref[...], everything[:, n].reshape(depth, width))
            left_all[part * COUNT + n] = both[:factor].astype(jnp.bfloat16)
            for piece in range(depth // 128):
                factor_rows[piece, pl.ds(p * COUNT + n, factor, residues), :] = both[
                    factor:, piece * 128 : (piece + 1) * 128
                ]

        @pl.when(p == half_parts - 1)
        def _():
            for e in range(factor):
                for piece in range(depth // 128):
                    right_all[r, e, :, piece * 128 : (piece + 1) * 128] = factor_rows[
                        piece, e * residues : e * residues + half, :
                    ].astype(jnp.bfloat16)

        update = attend_residues(
            gathered[q, pl.ds(part * COUNT, COUNT)],
            everything,
            wqg_ref[...],
            wkv_ref[...],
            wout_ref[...],
        )
        for n in range(COUNT):
            for piece in range(width // 128):
                strided[piece, pl.ds(part * COUNT + n, seqs, residues), :] = update[
                    n * seqs : (n + 1) * seqs, piece * 128 : (piece + 1) * 128
                ]

        @pl.when(p >= half_parts - 1)
        def _():
            advance(p - (half_parts - 1))

        return carry

    lax.fori_loop(0, parts, one_part, 0)

    def late(hop, carry):
        advance(hop)
        return carry

    lax.fori_loop(half_parts + 1, hops + 1, late, 0)

    def finish(i, carry):
        for piece in range(width // 128):
            o_ref[pl.ds(i * step, step), :, piece * 128 : (piece + 1) * 128] = (
                strided[piece, pl.ds(i * (step * residues), step * residues), :]
                .astype(jnp.bfloat16)
                .reshape(step, residues, 128)
            )
        return carry

    lax.fori_loop(0, seqs // step, finish, 0)

    for way in range(2):

        def shared(hop, carry):
            share_copy(way, hop, False).wait_recv()
            return carry

        lax.fori_loop(0, ways[way], shared, 0)

    pack = 128 // factor
    lanes = 2 * own_rows * factor
    left = jnp.concatenate(
        [
            left_all[pl.ds(q * own_rows, own_rows)].reshape(own_rows * factor, depth),
            left_all[pl.ds(across * own_rows, own_rows)].reshape(own_rows * factor, depth),
        ],
        axis=0,
    )
    each = outer.shape[0] // (lanes // 128) // half
    span = each * half
    turns = blocks // each

    def swap_copy(t):
        return send(
            outgoing.at[t], incoming.at[t], swap_send.at[t], swap_recv.at[t], (r, across)
        )

    def one_turn(t, carry):
        def one_block(b, inner):
            products = (
                mm_nt(right_all[t * each + b].reshape(factor * half, depth), left) * scaling
            ).astype(jnp.bfloat16)
            for e in range(factor):
                for g in range(lanes // 128):
                    outer[
                        pl.ds(pl.multiple_of(g * span + b * half, half), half),
                        e * 128 : (e + 1) * 128,
                    ] = products[e * half : (e + 1) * half, g * 128 : (g + 1) * 128]
            return inner

        lax.fori_loop(0, each, one_block, 0)
        pair = mm(outer[...], wpair_ref[...]).astype(jnp.bfloat16)

        def cut(i):
            g, k = i // pack, i % pack
            return pair[g * span : (g + 1) * span, k * channels : (k + 1) * channels]

        for i in range(own_rows):
            outgoing[t, i] = cut(own_rows + i)
        for i in range(own_rows):
            for b in range(each):
                start = pl.multiple_of((t * each + b) * residues + side * half, half)
                pair_ref[i, pl.ds(start, half), :] = cut(i)[b * half : (b + 1) * half]
        swap_copy(t).start()
        return carry

    lax.fori_loop(0, turns, one_turn, 0)

    def take(t, carry):
        swap_copy(t).wait_recv()
        for i in range(own_rows):
            for b in range(each):
                start = pl.multiple_of((t * each + b) * residues + (1 - side) * half, half)
                pair_ref[i, pl.ds(start, half), :] = incoming[t, i, b * half : (b + 1) * half, :]
        return carry

    lax.fori_loop(0, turns, take, 0)

    def drain(p, carry):
        cross(q, p, lax.rem(part_at(p) + half_parts, parts)).wait_send()
        direct(q, p, part_at(p)).wait_send()
        relay(across, p, part_at(p)).wait_send()
        return carry

    lax.fori_loop(0, parts, drain, 0)
    for way in range(2):

        def drain_ring(hop, carry):
            ring_copy(way, hop).wait_send()
            share_copy(way, hop).wait_send()
            return carry

        lax.fori_loop(0, ways[way], drain_ring, 0)

    def drain_swap(t, carry):
        swap_copy(t).wait_send()
        return carry

    lax.fori_loop(0, turns, drain_swap, 0)


def per_device(alignment, query_weight, w_keyval, w_gate, output_weight, w_factors, w_pair_out):
    seqs, residues, width = alignment.shape
    groups = lax.axis_size("seq")
    blocks = lax.axis_size("res")
    depth = seqs * groups
    factor = w_factors.shape[1] // 2
    channels = w_pair_out.shape[1]
    own_rows = residues // groups
    half = residues // 2
    parts = residues // COUNT
    hops = blocks // 2
    wft = jnp.transpose(w_factors)
    wqg = jnp.concatenate([query_weight, w_gate], axis=1)
    pack = 128 // factor
    w = jnp.transpose(w_pair_out.reshape(factor, factor, channels), (1, 0, 2))
    eye = jnp.eye(pack, dtype=w.dtype)
    spread = (w[:, None, :, None, :] * eye[None, :, None, :, None]).reshape(
        factor * pack * factor, pack * channels
    )
    each = math.gcd(blocks, 4)
    turns = blocks // each
    vmem = pl.BlockSpec(memory_space=pltpu.VMEM)
    dma = pltpu.SemaphoreType.DMA
    return pl.pallas_call(
        functools.partial(block_kernel, 1.0 / depth, blocks, groups),
        in_specs=[vmem] * 6,
        out_specs=[vmem] * 2,
        out_shape=[
            jax.ShapeDtypeStruct((seqs, residues, width), jnp.bfloat16),
            jax.ShapeDtypeStruct((own_rows, blocks * residues, channels), jnp.bfloat16),
        ],
        scratch_shapes=[
            pltpu.VMEM((groups, residues, seqs, width), jnp.bfloat16),
            pltpu.VMEM((width // 128, seqs * residues, 128), jnp.float32),
            pltpu.VMEM((depth // 128, factor * residues, 128), jnp.float32),
            pltpu.VMEM((residues, factor, depth), jnp.bfloat16),
            pltpu.VMEM((blocks, factor, half, depth), jnp.bfloat16),
            pltpu.VMEM((2 * own_rows * factor // 128 * each * half, factor * 128), jnp.bfloat16),
            pltpu.VMEM((turns, own_rows, each * half, channels), jnp.bfloat16),
            pltpu.VMEM((turns, own_rows, each * half, channels), jnp.bfloat16),
            dma((parts,)),
            dma((parts,)),
            dma((parts,)),
            dma((parts,)),
            dma((parts,)),
            dma((parts,)),
            dma((2, hops)),
            dma((2, hops)),
            dma((2, hops)),
            dma((2, hops)),
            dma((turns,)),
            dma((turns,)),
        ],
        compiler_params=pltpu.CompilerParams(
            vmem_limit_bytes=62 * 1024 * 1024, collective_id=0, has_side_effects=True
        ),
        name="block",
    )(alignment, wqg, w_keyval, output_weight, wft, spread)


def solution(mesh):
    in_specs = (P("seq", "res", None), P(), P(), P(), P(), P(), P())
    out_specs = (P("seq", "res", None), P(("res", "seq"), None, None))
    return jax.shard_map(
        per_device, mesh=mesh, in_specs=in_specs, out_specs=out_specs, check_vma=False
    )
```

time: 188 us -> 82.8 us (0.44)
  waiting for transfers between devices: 116 us -> 0 us
  Pallas kernels: 51.1 us -> 71.2 us
  between operations: 14.1 us -> 0.67 us
  local copies, waits for them, and re-layouts: 4.4 us -> 8.26 us
    all_gather x2 -> x0, waiting for transfers between devices: 116 us -> none  [the longest x1 66.4 us: per_device(): right_all = lax.all_gather(right, 'res', axis=0, tiled=False)]
    pallas_call x4 -> x1, Pallas kernels: 51.1 us -> 71.2 us  [per_device(): pl.pallas_call(functools.partial(block_kernel, 1.0 / depth, blocks, group...]
    unnamed x7, local copies, waits for them, and re-layouts: 2.67 us -> 7.21 us
  transfers between devices with their start and end apart: 2 -> 0, of which waited for: 2 -> 0; matrix products, arithmetic and copies ran while one was open for 4% -> 0% of each run, Pallas kernels for 14% -> 0%
where the time goes in v2:
time: 82.8 us; the launch traced here: 82.5 us
  Pallas kernels  71.2 us (86%)
  local copies, waits for them, and re-layouts  8.26 us (10%)
  other arithmetic  2.38 us (3%)
    pallas_call x1, Pallas kernels, per_device(): pl.pallas_call(functools.partial(block_kernel, 1.0 / depth, blocks, group...  71.2 us
    unnamed x7, local copies, waits for them, and re-layouts  7.21 us

profile of v2, /device:TPU:0, one launch (start us, length us, event | category | flops | bytes accessed | tf_op | source)
XLA Modules:
  0.0 82.5 jit_solution(8446779592657280829)
XLA Ops:
  0.6 1.1 %copy.9 = bf16[32,32,128]{2,1,0:T(8,128)(2,1)S(1)} copy(bf16[32,32,128]{2,0,1:T(8,128)(2,1)} %bitcast.11) | data formatting | bytes 524288 | tf_op jit(solution)/shard_map/transpose | solution.py:412
  1.7 1.6 %broadcast_multiply_fusion = bf16[32,4,32,4,128]{4,3,2,1,0:T(4,128)(2,1)S(1)} fusion(bf16[4,4]{1,0:T(4,128)(2,1)S(1)} %fusion, bf16[32,32,128]{2,1,0:T(8,128)(2,1)S(1)} %copy.9), kind=kLoop, calls=%fused_computation.1 | loop fusion | flops 2097152 | bytes 4456480 | tf_op jit(solution)/shard_map/mul | solution.py:414
  3.4 0.0 copy-start
  3.4 0.0 copy-start.1
  3.4 2.7 %copy.12 = bf16[512,8,4,128]{3,1,2,0:T(8,128)(2,1)} copy(bf16[512,8,4,128]{3,2,1,0:T(4,128)(2,1)S(1)} %bitcast.10) | data formatting | bytes 8388608
  6.0 0.0 copy-done
  6.0 0.0 copy-done.1
  6.0 0.7 pad_maximum_fusion.wqg_ref
  6.8 71.2 %block.1 = (bf16[96,32,256]{2,1,0:T(8,128)(2,1)}, bf16[8,256,128]{2,1,0:T(8,128)(2,1)}) custom-call(bf16[96,32,256]{2,1,0:T(8,128)(2,1)} %x_ref.1, bf16[256,512]{1,0:T(8,128)(2,1)} %pad_maximum_fusion.wqg_ref, bf16[256,512]{1,0:T(8,128)(2,1)} %wkv_ref.1, bf16[256,256]{1,0:T(8,128)(2,1)} %wout_ref.1, bf16[64,256]{1,0:T(8,128)(2,1)} %bitcast.12, ...), custom_call_target="tpu_custom_call" | custom-call | tf_op jit(solution)/shard_map/block/pallas_call | solution.py:421
  78.0 2.7 %copy.15 = bf16[96,32,256]{2,1,0:T(8,128)(2,1)} copy(bf16[96,32,256]{2,1,0:T(8,128)(2,1)} %get-tuple-element.4) | data formatting | bytes 3145728
  80.7 1.9 %copy.16 = bf16[8,256,128]{2,1,0:T(8,128)(2,1)} copy(bf16[8,256,128]{2,1,0:T(8,128)(2,1)} %get-tuple-element.5) | data formatting | bytes 1048576
  (1 shorter events, 0.0 us)
Async XLA Ops:
  3.4 2.7 %copy-start = (bf16[256,256]{1,0:T(8,128)(2,1)S(1)}, bf16[256,256]{1,0:T(8,128)(2,1)}, u32[]{:S(2)}) copy-start(bf16[256,256]{1,0:T(8,128)(2,1)} %param.10) | copy-start | bytes 393220
  3.4 2.7 %copy-start.1 = (bf16[256,256]{1,0:T(8,128)(2,1)S(1)}, bf16[256,256]{1,0:T(8,128)(2,1)}, u32[]{:S(2)}) copy-start(bf16[256,256]{1,0:T(8,128)(2,1)} %param.8) | copy-start | bytes 393220

commit v3 on v2

v3 whole, which is shorter than its diff:
```python
import functools
import math

import jax
import jax.numpy as jnp
from jax import lax
from jax.experimental import pallas as pl
from jax.experimental.pallas import tpu as pltpu
from jax.sharding import PartitionSpec as P

HEADS = 8
HC = 32
LOG2E = 1.4426950408889634
epsilon = 1e-05
NT = (((1,), (1,)), ((), ()))


def mm(a, b):
    return jnp.dot(a, b, preferred_element_type=jnp.float32)


def mm_nt(a, b):
    return lax.dot_general(a, b, NT, preferred_element_type=jnp.float32)


MESH = pl.DeviceIdType.MESH
COUNT = 4


def attend_residues(own, everything, wq, wg, wkv, wout):
    groups, count, seqs, width = everything.shape
    hidden = HEADS * HC
    kv = mm(everything.reshape(groups * count * seqs, width), wkv).astype(jnp.bfloat16)
    kv = kv.reshape(groups, count, seqs, 2 * hidden)
    rows = own.reshape(count * seqs, width)
    queries = mm(rows, wq).astype(jnp.bfloat16)
    gating = jax.nn.sigmoid(mm(rows, wg))
    head_of = lax.broadcasted_iota(jnp.int32, (seqs, hidden), 1) // HC
    gated = []
    for n in range(count):
        q = queries[n * seqs : (n + 1) * seqs].astype(jnp.float32)
        stacked = jnp.concatenate(
            [jnp.where(head_of == h, q, 0.0).astype(jnp.bfloat16) for h in range(HEADS)], axis=0
        )
        keys = kv[:, n, :, :hidden].reshape(groups * seqs, hidden)
        values = kv[:, n, :, hidden:].reshape(groups * seqs, hidden)
        exponent = jnp.exp2(mm_nt(stacked, keys) * (LOG2E / math.sqrt(HC)))
        inverse = 1.0 / jnp.sum(exponent, axis=-1, keepdims=True)
        weighted = mm(exponent.astype(jnp.bfloat16), values)
        attended = jnp.zeros((seqs, hidden), jnp.float32)
        for h in range(HEADS):
            rows = slice(h * seqs, (h + 1) * seqs)
            attended = jnp.where(head_of == h, weighted[rows] * inverse[rows], attended)
        gated.append((gating[n * seqs : (n + 1) * seqs] * attended).astype(jnp.bfloat16))
    return mm(jnp.concatenate(gated, axis=0), wout)


def block_kernel(
    scaling,
    blocks,
    groups,
    x_ref,
    wq_ref,
    wkv_ref,
    wg_ref,
    wout_ref,
    wf_ref,
    wp_ref,
    o_ref,
    pair_ref,
    gathered,
    strided,
    pair_rows,
    spread,
    wft,
    left_all,
    right_all,
    products,
    outer,
    outgoing,
    incoming,
    cross_send,
    cross_recv,
    twin_send,
    twin_recv,
    relay_send,
    relay_recv,
    ring_send,
    ring_recv,
    share_send,
    share_recv,
    swap_send,
    swap_recv,
):
    seqs, residues, width = x_ref.shape
    depth = seqs * groups
    factor = wf_ref.shape[1] // 2
    pack = 128 // factor
    own_rows = residues // groups
    channels = pair_ref.shape[2]
    half = residues // 2
    parts = residues // COUNT
    half_parts = parts // 2
    hops = blocks // 2
    r = lax.axis_index("res")
    q = lax.axis_index("seq")
    core = lax.rem(q, 2)
    side = q // 2
    twin = q + 1 - 2 * core
    across = lax.rem(q + 2, groups)
    twin_across = lax.rem(twin + 2, groups)

    def ring_of(block):
        z, y = block // 2, lax.rem(block, 2)
        return jnp.where(y == 0, z, blocks - 1 - z)

    def block_of(place):
        return jnp.where(place < blocks // 2, 2 * place, 2 * (blocks - 1 - place) + 1)

    place = ring_of(r)
    ahead = block_of(lax.rem(place + 1, blocks))
    behind = block_of(lax.rem(place + blocks - 1, blocks))

    barrier = pltpu.get_barrier_semaphore()
    for target in ((r, twin), (r, across), (ahead, q), (behind, q)):
        pl.semaphore_signal(barrier, inc=1, device_id=target, device_id_type=MESH)
    pl.semaphore_wait(barrier, 4)

    def part_at(p):
        return lax.rem(p + side * half_parts, parts)

    def rows_of(owner, part):
        return gathered.at[owner, pl.ds(part * COUNT, COUNT)]

    def send(ref, dst, send_sem, recv_sem, target):
        return pltpu.make_async_remote_copy(
            src_ref=ref,
            dst_ref=dst,
            send_sem=send_sem,
            recv_sem=recv_sem,
            device_id=target,
            device_id_type=MESH,
        )

    def cross(owner, p, part):
        block = rows_of(owner, part)
        return send(block, block, cross_send.at[p], cross_recv.at[p], (r, across))

    def direct(owner, p, part):
        block = rows_of(owner, part)
        return send(block, block, twin_send.at[p], twin_recv.at[p], (r, twin))

    def relay(owner, p, part):
        block = rows_of(owner, part)
        return send(block, block, relay_send.at[p], relay_recv.at[p], (r, twin))

    step = 8
    for turn in range(2):
        which = (1 - side) if turn == 0 else side
        base = pl.multiple_of(which * half, half)

        def norm(i, carry):
            values = (
                x_ref[pl.ds(i * step, step), pl.ds(base, half), :]
                .reshape(step * half, width)
                .astype(jnp.float32)
            )
            centered = values - jnp.mean(values, axis=-1, keepdims=True)
            spread = jnp.mean(centered * centered, axis=-1, keepdims=True)
            normed = centered * lax.rsqrt(spread + epsilon)
            for part in range(width // 128):
                strided[part, pl.ds(i * (step * half), step * half), :] = normed[
                    :, part * 128 : (part + 1) * 128
                ]
            return carry

        lax.fori_loop(0, seqs // step, norm, 0)

        def move(k, carry):
            for n in range(COUNT):
                for part in range(width // 128):
                    gathered[q, base + k * COUNT + n, :, part * 128 : (part + 1) * 128] = strided[
                        part, pl.ds(k * COUNT + n, seqs, half), :
                    ].astype(jnp.bfloat16)
            return carry

        def start_across(k, carry):
            cross(q, turn * half_parts + k, which * half_parts + k).start()
            return carry

        def move_and_start(k, carry):
            move(k, carry)
            return start_across(k, carry)

        lax.fori_loop(0, half_parts, move_and_start, 0)

    def start_twin(p, carry):
        direct(q, p, part_at(p)).start()
        return carry

    lax.fori_loop(0, parts, start_twin, 0)

    both_factors = 2 * factor
    unit = jnp.where(
        lax.broadcasted_iota(jnp.int32, (both_factors, both_factors), 0)
        == lax.broadcasted_iota(jnp.int32, (both_factors, both_factors), 1),
        1.0,
        0.0,
    ).astype(jnp.bfloat16)
    wft[...] = mm_nt(unit, wf_ref[...]).astype(jnp.bfloat16)
    pair_rows[...] = wp_ref[...].astype(jnp.float32)
    spread[...] = jnp.zeros_like(spread)
    for e in range(factor):
        rows = pair_rows[pl.ds(e, factor, factor), :].astype(jnp.bfloat16)
        for k in range(pack):
            start = (e * pack + k) * factor
            spread[start : start + factor, k * channels : (k + 1) * channels] = rows

    share = COUNT // 2

    def mine(sub):
        return pl.ds(sub * COUNT + core * share, share)

    def twins(sub):
        return pl.ds(sub * COUNT + (1 - core) * share, share)

    def ring_copy(way, sub, hop):
        shift = blocks - hop if way == 0 else hop
        block = block_of(lax.rem(place + shift, blocks))
        ref = right_all.at[block, mine(sub)]
        return send(
            ref,
            ref,
            ring_send.at[way, sub, hop],
            ring_recv.at[way, sub, hop],
            ((ahead if way == 0 else behind), q),
        )

    def landed(way, hop):
        shift = blocks - hop - 1 if way == 0 else hop + 1
        return block_of(lax.rem(place + shift, blocks))

    def arrive(way, sub, hop):
        ref = right_all.at[landed(way, hop), mine(sub)]
        send(
            ref,
            ref,
            ring_send.at[way, sub, hop],
            ring_recv.at[way, sub, hop],
            ((ahead if way == 0 else behind), q),
        ).wait_recv()

    def share_copy(way, sub, hop, outward=True):
        ref = right_all.at[landed(way, hop), mine(sub) if outward else twins(sub)]
        return send(
            ref, ref, share_send.at[way, sub, hop], share_recv.at[way, sub, hop], (r, twin)
        )

    ways = (hops, blocks - 1 - hops)

    def advance(sub, hop):
        for way in range(2):

            @pl.when((hop > 0) & (hop <= ways[way]))
            def _():
                arrive(way, sub, hop - 1)

            @pl.when((hop >= 0) & (hop < ways[way]))
            def _():
                ring_copy(way, sub, hop).start()

            @pl.when((hop > 0) & (hop <= ways[way]))
            def _():
                share_copy(way, sub, hop - 1).start()

    def advance_all(p):
        for sub in range(half_parts):
            advance(sub, p - sub)

    def one_part(p, carry):
        part = part_at(p)
        cross(across, p, part).wait_recv()
        relay(across, p, part).start()
        direct(twin, p, part).wait_recv()
        relay(twin_across, p, part).wait_recv()
        everything = gathered[:, pl.ds(part * COUNT, COUNT)]
        for n in range(COUNT):
            both = mm_nt(wft[...], everything[:, n].reshape(depth, width)).astype(jnp.bfloat16)
            left_all[part * COUNT + n] = both[:factor]

            @pl.when(p < half_parts)
            def _():
                right_all[r, p * COUNT + n] = both[factor:]

        update = attend_residues(
            gathered[q, pl.ds(part * COUNT, COUNT)],
            everything,
            wq_ref[...],
            wg_ref[...],
            wkv_ref[...],
            wout_ref[...],
        )
        for n in range(COUNT):
            for piece in range(width // 128):
                strided[piece, pl.ds(part * COUNT + n, seqs, residues), :] = update[
                    n * seqs : (n + 1) * seqs, piece * 128 : (piece + 1) * 128
                ]

        advance_all(p)
        return carry

    lax.fori_loop(0, parts, one_part, 0)

    def late(p, carry):
        advance_all(p)
        return carry

    lax.fori_loop(parts, half_parts + hops, late, 0)

    for way in range(2):
        for sub in range(half_parts):

            def shared(hop, carry):
                share_copy(way, sub, hop, False).wait_recv()
                return carry

            lax.fori_loop(0, ways[way], shared, 0)

    lanes = own_rows * factor
    span = blocks * half

    def pair_of(owner):
        left = left_all[pl.ds(owner * own_rows, own_rows)].reshape(lanes, depth)

        def one_block(b, inner):
            value = mm_nt(right_all[b].reshape(half * factor, depth), left) * scaling
            for g in range(lanes // 128):
                products[g] = value[:, g * 128 : (g + 1) * 128]
            for e in range(factor):
                for g in range(lanes // 128):
                    outer[
                        pl.ds(pl.multiple_of(g * span + b * half, half), half),
                        e * 128 : (e + 1) * 128,
                    ] = products[g, pl.ds(e, half, factor), :].astype(jnp.bfloat16)
            return inner

        lax.fori_loop(0, blocks, one_block, 0)
        return mm(outer[...], spread[...]).astype(jnp.bfloat16)

    def cut(pair, i):
        g, k = i // pack, i % pack
        return pair[g * span : (g + 1) * span, k * channels : (k + 1) * channels]

    def swap_copy():
        return send(outgoing, incoming, swap_send, swap_recv, (r, across))

    pair = pair_of(across)
    for i in range(own_rows):
        outgoing[i] = cut(pair, i)
    swap_copy().start()

    def place_rows(i, which, value):
        for b in range(blocks):
            start = pl.multiple_of(b * residues + which * half, half)
            pair_ref[i, pl.ds(start, half), :] = value[b * half : (b + 1) * half]

    pair = pair_of(q)
    for i in range(own_rows):
        place_rows(i, side, cut(pair, i))

    def finish(i, carry):
        for piece in range(width // 128):
            o_ref[pl.ds(i * step, step), :, piece * 128 : (piece + 1) * 128] = (
                strided[piece, pl.ds(i * (step * residues), step * residues), :]
                .astype(jnp.bfloat16)
                .reshape(step, residues, 128)
            )
        return carry

    lax.fori_loop(0, seqs // step, finish, 0)
    swap_copy().wait_recv()
    for i in range(own_rows):
        place_rows(i, 1 - side, incoming[i])

    def drain(p, carry):
        cross(q, p, lax.rem(part_at(p) + half_parts, parts)).wait_send()
        direct(q, p, part_at(p)).wait_send()
        relay(across, p, part_at(p)).wait_send()
        return carry

    lax.fori_loop(0, parts, drain, 0)
    for way in range(2):
        for sub in range(half_parts):

            def drain_ring(hop, carry):
                ring_copy(way, sub, hop).wait_send()
                share_copy(way, sub, hop).wait_send()
                return carry

            lax.fori_loop(0, ways[way], drain_ring, 0)
    swap_copy().wait_send()


def per_device(alignment, query_weight, w_keyval, w_gate, output_weight, w_factors, w_pair_out):
    seqs, residues, width = alignment.shape
    groups = lax.axis_size("seq")
    blocks = lax.axis_size("res")
    depth = seqs * groups
    factor = w_factors.shape[1] // 2
    channels = w_pair_out.shape[1]
    own_rows = residues // groups
    half = residues // 2
    parts = residues // COUNT
    hops = blocks // 2
    pack = 128 // factor
    subs = parts // 2
    span = blocks * half
    vmem = pl.BlockSpec(memory_space=pltpu.VMEM)
    dma = pltpu.SemaphoreType.DMA
    return pl.pallas_call(
        functools.partial(block_kernel, 1.0 / depth, blocks, groups),
        in_specs=[vmem] * 7,
        out_specs=[vmem] * 2,
        out_shape=[
            jax.ShapeDtypeStruct((seqs, residues, width), jnp.bfloat16),
            jax.ShapeDtypeStruct((own_rows, blocks * residues, channels), jnp.bfloat16),
        ],
        scratch_shapes=[
            pltpu.VMEM((groups, residues, seqs, width), jnp.bfloat16),
            pltpu.VMEM((width // 128, seqs * residues, 128), jnp.float32),
            pltpu.VMEM((factor * factor, channels), jnp.float32),
            pltpu.VMEM((factor * 128, pack * channels), jnp.bfloat16),
            pltpu.VMEM((2 * factor, width), jnp.bfloat16),
            pltpu.VMEM((residues, factor, depth), jnp.bfloat16),
            pltpu.VMEM((blocks, half, factor, depth), jnp.bfloat16),
            pltpu.VMEM((own_rows // pack, half * factor, 128), jnp.float32),
            pltpu.VMEM((own_rows // pack * span, factor * 128), jnp.bfloat16),
            pltpu.VMEM((own_rows, span, channels), jnp.bfloat16),
            pltpu.VMEM((own_rows, span, channels), jnp.bfloat16),
            dma((parts,)),
            dma((parts,)),
            dma((parts,)),
            dma((parts,)),
            dma((parts,)),
            dma((parts,)),
            dma((2, subs, hops)),
            dma((2, subs, hops)),
            dma((2, subs, hops)),
            dma((2, subs, hops)),
            dma,
            dma,
        ],
        compiler_params=pltpu.CompilerParams(
            vmem_limit_bytes=62 * 1024 * 1024, collective_id=0, has_side_effects=True
        ),
        name="block",
    )(alignment, query_weight, w_keyval, w_gate, output_weight, w_factors, w_pair_out)


def solution(mesh):
    in_specs = (P("seq", "res", None), P(), P(), P(), P(), P(), P())
    out_specs = (P("seq", "res", None), P(("res", "seq"), None, None))
    return jax.shard_map(
        per_device, mesh=mesh, in_specs=in_specs, out_specs=out_specs, check_vma=False
    )
```

time: 82.8 us -> 79.4 us (0.959)
  local copies, waits for them, and re-layouts: 8.26 us -> 5.02 us
  other arithmetic: 2.38 us -> 0 us
  Pallas kernels: 71.2 us -> 73.5 us
    pallas_call x1, Pallas kernels: 71.2 us -> 73.5 us  [per_device(): pl.pallas_call(functools.partial(block_kernel, 1.0 / depth, blocks, group...]
    unnamed x7 -> x5, local copies, waits for them, and re-layouts: 7.21 us -> 5.02 us
    mul x1 -> x0, other arithmetic: 1.65 us -> none  [per_device(): w[:, None, :, None, :] * eye[None, :, None, :, None]]
    transpose x1 -> x0, local copies, waits for them, and re-layouts: 1.06 us -> none  [per_device(): w = jnp.transpose(w_pair_out.reshape(factor, factor, channels), (1, 0, 2))]
where the time goes in v3:
time: 79.4 us; the launch traced here: 79.2 us
  Pallas kernels  73.5 us (93%)
  local copies, waits for them, and re-layouts  5.02 us (6%)
    pallas_call x1, Pallas kernels, per_device(): pl.pallas_call(functools.partial(block_kernel, 1.0 / depth, blocks, group...  73.5 us
    unnamed x5, local copies, waits for them, and re-layouts  5.02 us

profile of v3, /device:TPU:0, one launch (start us, length us, event | category | flops | bytes accessed | tf_op | source)
XLA Modules:
  0.0 79.2 jit_solution(8916651555155443279)
XLA Ops:
  0.6 1.5 %copy.9.wf_ref = bf16[256,64]{1,0:T(8,128)(2,1)} copy(bf16[256,64]{0,1:T(8,128)(2,1)} %param.12) | data formatting | bytes 65536 | tf_op args[5]
  2.1 73.5 %block.1 = (bf16[96,32,256]{2,1,0:T(8,128)(2,1)}, bf16[8,256,128]{2,1,0:T(8,128)(2,1)}) custom-call(bf16[96,32,256]{2,1,0:T(8,128)(2,1)} %x_ref.1, bf16[256,256]{1,0:T(8,128)(2,1)} %wq_ref.1, bf16[256,512]{1,0:T(8,128)(2,1)} %wkv_ref.1, bf16[256,256]{1,0:T(8,128)(2,1)} %wg_ref.1, bf16[256,256]{1,0:T(8,128)(2,1)} %wout_ref.1, bf16[256,64]{1,0:T(8,128)(2,1)} %copy.9.wf_ref, ...), custom_call_target="tpu_custom_call" | custom-call | tf_op jit(solution)/shard_map/block/pallas_call | solution.py:420
  75.6 0.0 copy-start
  75.6 2.7 %copy.12 = bf16[96,32,256]{2,1,0:T(8,128)(2,1)} copy(bf16[96,32,256]{2,1,0:T(8,128)(2,1)} %get-tuple-element.4) | data formatting | bytes 3145728
  78.4 0.0 copy-done
  78.4 0.8 %copy.13 = bf16[8,256,128]{2,1,0:T(8,128)(2,1)} copy(bf16[8,256,128]{2,1,0:T(8,128)(2,1)S(1)} %copy-done) | data formatting | bytes 1048576
Async XLA Ops:
  75.6 2.7 %copy-start = (bf16[8,256,128]{2,1,0:T(8,128)(2,1)S(1)}, bf16[8,256,128]{2,1,0:T(8,128)(2,1)}, u32[]{:S(2)}) copy-start(bf16[8,256,128]{2,1,0:T(8,128)(2,1)} %get-tuple-element.5) | copy-start | bytes 1572868
